TPU v7x, 512 devices: a whole 4x4x16 slice. The times are simulated.
512 devices in a mesh: box: 16 (over x, y_hi, core), sib: 2 (over y_lo), grp: 16 (over z).
Axes of the slice: x: 4, y: 4 (y_hi: 2, y_lo: 2; y = y_hi * 2 + y_lo), z: 16, core: 2. Of those that a mesh axis runs over, the one named last changes fastest.
Arguments:
- interface_maps: float32 [2, 32, 1024, 1024], P('sib', 'box', 'grp'), parts along dimension 1, may hold values from -1 to 1
- pivot_inverses: float32 [2, 32, 512, 512], P('sib', 'box', None, 'grp'), parts along dimension 1, may hold values from -1 to 5
- exterior_coupling: float32 [32, 1024, 5120], P('box', 'sib', 'grp'), parts along dimension 0, may hold values from -1 to 1
- face_blocks: int32 [32, 8], P('box'), parts along dimension 0, may hold values from 0 to 7, each once within a row
Outputs:
- interface_schur: float32 [32, 1024, 1024], P('box', 'sib', 'grp'), parts along dimension 0
- exterior_update: float32 [32, 1024, 5120], P('box', 'sib', 'grp'), parts along dimension 0
- multipliers: float32 [32, 1024, 1024], P('box', 'grp', 'sib'), parts along dimension 0
There are 16 independent parts, one for each index of `box`. A program takes and returns all parts, laid end to end along the dimension named above; each array names one. Nothing has to cross between parts.
Inputs may be any that keep to these rules, and one draw needn't show every extreme that they name: `face_blocks`: each row is an ordering of the 8 blocks of one child: row 0 for the first child, row 1 for the second.
All inputs are finite; a program needn't handle non-finite values.
Results may differ from a plain program's by a relative error of at most 0.0001.
Values sent between devices are 32-bit elements; how exact they have to be, the bound alone decides.
A program may use at most 128 MiB of HBM per device.

v0:
```python
import jax
import jax.numpy as jnp
from jax import lax
from jax.sharding import PartitionSpec as P


def partner(block, axis, bit):
    count = lax.axis_size(axis)
    route = []
    for low in range(count):
        high = low | 1 << bit
        if high != low and high < count:
            route += [(low, high), (high, low)]
    return lax.ppermute(block, axis, route)


def in_blocks(shard, dim, count):
    dims = shard.shape
    pieces = shard.reshape(*dims[:dim], count, dims[dim] // count, *dims[dim + 1 :])
    return jnp.moveaxis(pieces, dim, 0)


def summed_on_arrival(shard, axis, dim):
    pieces = in_blocks(shard, dim, lax.axis_size(axis))
    arrived = lax.all_to_all(pieces, axis, split_axis=0, concat_axis=0, tiled=True)
    return arrived.sum(axis=0)


def in_one_piece(arrays, axis, dim, along):
    ends, at = ([], 0)
    for a in arrays[:-1]:
        at += a.shape[along]
        ends.append(at)
    both = jnp.concatenate(arrays, axis=along)
    return tuple(jnp.split(summed_on_arrival(both, axis, dim), ends, axis=along))


def complex_dot(left_side, right_side):

    def product(first_part, second_part):
        return jnp.dot(
            first_part,
            second_part,
            precision=lax.Precision.HIGHEST,
            preferred_element_type=jnp.float32,
        )

    real_part = product(left_side[0], right_side[0]) - product(left_side[1], right_side[1])
    imag_part = product(left_side[0], right_side[1]) + product(left_side[1], right_side[0])
    return jnp.stack([real_part, imag_part])


def block_sources(face_blocks):
    alpha_order = face_blocks[0]
    beta_order = face_blocks[1]
    slots = jnp.arange(face_blocks.shape[1], dtype=jnp.int32)
    beta_match = (beta_order[:, None] == slots[None, :]).astype(jnp.int32)
    alpha_match = (alpha_order[:, None] == slots[None, :]).astype(jnp.int32)
    to_beta = jnp.sum(beta_match * alpha_order[:, None], axis=0)
    to_alpha = jnp.sum(alpha_match * beta_order[:, None], axis=0)
    return (to_beta, to_alpha)


def reorder(matrix, source):
    blocks = source.shape[0]
    grouped = matrix.reshape(matrix.shape[0], blocks, matrix.shape[1] // blocks, matrix.shape[2])
    return jnp.take(grouped, source, axis=1).reshape(matrix.shape)


def per_device(interface_maps, pivot_inverses, exterior_coupling, face_blocks):
    own_rows = interface_maps[0]
    partner_rows = partner(own_rows, "sib", 0)
    sibling = lax.axis_index("sib")
    member = lax.axis_index("grp")
    alpha_rows = jnp.where(sibling == 0, own_rows, partner_rows)
    beta_rows = jnp.where(sibling == 0, partner_rows, own_rows)
    local_rows = own_rows.shape[1]
    order_size = own_rows.shape[2]
    panel_width = pivot_inverses.shape[2]
    half_rows = order_size // 2
    to_beta, to_alpha = block_sources(face_blocks)
    panel_section = lax.dynamic_slice_in_dim(alpha_rows, sibling * panel_width, panel_width, 2)
    raw_multipliers = complex_dot(
        panel_section, lax.all_gather(pivot_inverses, "grp", axis=3, tiled=True)[0]
    )
    beta_cols = lax.all_to_all(beta_rows, "grp", split_axis=2, concat_axis=1, tiled=True)
    beta_perm = reorder(beta_cols, to_alpha)
    local_cols = beta_perm.shape[2]
    beta_panel = lax.dynamic_slice_in_dim(beta_perm, sibling * panel_width, panel_width, 1)
    piece = lax.all_gather(raw_multipliers, "grp", axis=1, tiled=True)
    joined = jnp.concatenate(
        [piece, -complex_dot(piece, beta_panel), complex_dot(piece, exterior_coupling)], axis=2
    )
    joined = reorder(joined, to_beta)
    multipliers = lax.dynamic_slice_in_dim(
        joined[:, :, :panel_width], member * local_rows, local_rows, 1
    )
    partial_schur = joined[:, :, panel_width : panel_width + local_cols]
    partial_exterior = joined[:, :, panel_width + local_cols :]
    summed_schur, exterior_update = in_one_piece((partial_schur, partial_exterior), "sib", 1, 2)
    row_index = sibling * half_rows + jnp.arange(half_rows, dtype=jnp.int32)
    col_index = member * local_cols + jnp.arange(local_cols, dtype=jnp.int32)
    identity_real = (row_index[:, None] == col_index[None, :]).astype(jnp.float32)
    identity_block = jnp.stack([identity_real, jnp.zeros_like(identity_real)])
    interface_schur = identity_block + summed_schur
    return (interface_schur, exterior_update, multipliers)


def solution(mesh):
    in_specs = (
        P("sib", "box", "grp", None),
        P("sib", "box", None, "grp"),
        P("box", "sib", "grp"),
        P("box", None),
    )
    out_specs = (P("box", "sib", "grp"), P("box", "sib", "grp"), P("box", "grp", "sib"))
    return jax.shard_map(
        per_device, mesh=mesh, in_specs=in_specs, out_specs=out_specs, check_vma=False
    )
```

profile of v0, /device:TPU:6, one launch (start us, length us, event | category | flops | bytes accessed | tf_op | source)
XLA Modules:
  0.0 276.9 jit_solution(12519139690456995614)
XLA Ops:
  7.9 3.5 %collective-permute-start = (f32[2,64,1024]{2,1,0:T(8,128)}, f32[2,64,1024]{2,1,0:T(8,128)S(1)}, u32[]{:S(2)}, u32[]{:S(2)}) collective-permute-start(f32[2,64,1024]{2,1,0:T(8,128)} %bitcast.121), channel_id=1, source_target_pairs={{0,16},{16,0},{1,17},{17,1},{2,18},{18,2},{3,19},{19,3},{4,20},{20... | collective-permute-start | bytes 1572872 | tf_op jit(solution)/shard_map/ppermute | solution.py:14
  11.4 12.3 %collective-permute-done = f32[2,64,1024]{2,1,0:T(8,128)S(1)} collective-permute-done((f32[2,64,1024]{2,1,0:T(8,128)}, f32[2,64,1024]{2,1,0:T(8,128)S(1)}, u32[]{:S(2)}, u32[]{:S(2)}) %collective-permute-start) | collective-permute-done | bytes 524320 | tf_op jit(solution)/shard_map/ppermute | solution.py:14
  24.7 62.4 %all-gather.3.cloned.1.call-done = f32[1,2,512,512]{2,3,1,0:T(8,128)} async-done(((f32[1,2,512,32]{2,3,1,0:T(8,128)}), f32[1,2,512,512]{2,3,1,0:T(8,128)}) %all-gather.3.cloned.1.call-update) | async-done | bytes 2097168 | tf_op jit(solution)/shard_map/all_gather | solution.py:84
  87.1 2.5 fusion.19
  89.6 2.3 fusion.18
  97.5 8.0 %all-to-all-start = ((f32[16,1,8192]{2,1,0:T(1,128)}), f32[16,1,8192]{2,1,0:T(1,128)S(1)}, u32[]{:S(2)}, u32[]{:S(2)}) async-start(f32[16,1,8192]{2,1,0:T(1,128)} %reshape.137), calls=%async_computation | async-start | bytes 1048576 | tf_op jit(solution)/shard_map/all_to_all | solution.py:86
  105.8 24.2 %all-to-all-done = f32[16,1,8192]{2,1,0:T(1,128)S(1)} async-done(((f32[16,1,8192]{2,1,0:T(1,128)}), f32[16,1,8192]{2,1,0:T(1,128)S(1)}, u32[]{:S(2)}, u32[]{:S(2)}) %all-to-all-start) | async-done | bytes 524320 | tf_op jit(solution)/shard_map/all_to_all | solution.py:86
  134.8 43.9 %all-gather.5.cloned.1.call-done = f32[2,1024,512]{2,1,0:T(8,128)} async-done(((f32[2,64,512]{2,1,0:T(8,128)}), f32[2,1024,512]{2,1,0:T(8,128)}) %all-gather.5.cloned.1.call-update) | async-done | bytes 4194320 | tf_op jit(solution)/shard_map/all_gather | solution.py:90
  178.8 3.9 %fusion.3 = f32[1024,64]{0,1:T(8,128)S(1)} fusion(f32[2,1024,512]{2,1,0:T(8,128)} %all-gather.5.cloned.1.call-done, f32[2,512,64]{1,2,0:T(8,128)S(1)} %dynamic-slice_select_fusion), kind=kOutput, calls=%fused_computation.10 | convolution fusion | flops 402653184 | bytes 2490368 | tf_op jit(solution)/shard_map/dot_general | solution.py:41
  182.7 3.7 %fusion.2 = f32[1024,64]{0,1:T(8,128)S(1)} fusion(f32[2,1024,512]{2,1,0:T(8,128)} %all-gather.5.cloned.1.call-done, f32[2,512,64]{1,2,0:T(8,128)S(1)} %dynamic-slice_select_fusion), kind=kOutput, calls=%fused_computation.9 | convolution fusion | flops 402653184 | bytes 2490368 | tf_op jit(solution)/shard_map/dot_general | solution.py:41
  186.4 2.2 fusion.13
  188.6 2.2 fusion.15
  192.1 4.3 %fusion.1 = f32[1024,320]{0,1:T(8,128)S(1)} fusion(f32[2,1024,512]{2,1,0:T(8,128)} %all-gather.5.cloned.1.call-done, f32[2,512,320]{1,2,0:T(8,128)S(1)} %copy-done.4), kind=kOutput, calls=%fused_computation.8 | convolution fusion | flops 2013265920 | bytes 4063232 | tf_op jit(solution)/shard_map/dot_general | solution.py:41
  196.4 3.9 %fusion = f32[1024,320]{0,1:T(8,128)S(1)} fusion(f32[2,1024,512]{2,1,0:T(8,128)} %all-gather.5.cloned.1.call-done, f32[2,512,320]{1,2,0:T(8,128)S(1)} %copy-done.4), kind=kOutput, calls=%fused_computation.7 | convolution fusion | flops 2013265920 | bytes 4063232 | tf_op jit(solution)/shard_map/dot_general | solution.py:41
  200.4 2.4 fusion.9
  202.8 2.4 fusion.11
  206.9 2.3 copy.111
  209.2 5.5 %pad_maximum_fusion = f32[2,1024,896]{2,1,0:T(8,128)} fusion(f32[2,1024,320]{2,1,0:T(8,128)S(1)} %copy.111, f32[2,1024,64]{2,1,0:T(8,128)} %copy.110, f32[2,1024,512]{2,1,0:T(8,128)} %all-gather.5.cloned.1.call-done), kind=kLoop, calls=%fused_computation.2 | loop fusion | flops 3670016 | bytes 14680064 | tf_op jit(solution)/shard_map/concatenate | solution.py:91
  214.7 7.1 %gather_fusion.1 = f32[8,2,128,896]{3,2,1,0:T(8,128)} fusion(f32[2,8,128,896]{3,2,1,0:T(8,128)} %bitcast.116, s32[1024]{0:T(1024)S(1)} %pad_clamp_fusion), kind=kCustom, calls=%fused_computation.1 | custom fusion | bytes 14680096 | tf_op jit(solution)/shard_map/jit(_take)/gather | solution.py:67
  221.8 3.8 %copy.112 = f32[2,8,128,896]{3,2,1,0:T(8,128)S(1)} copy(f32[2,8,128,896]{3,2,0,1:T(8,128)} %bitcast.115) | data formatting | bytes 14680064 | tf_op jit(solution)/shard_map/jit(_take)/gather | solution.py:67
  226.1 2.9 %copy-done.2 = f32[2,1024,896]{2,1,0:T(8,128)} copy-done((f32[2,1024,896]{2,1,0:T(8,128)}, f32[2,1024,896]{2,1,0:T(8,128)S(1)}, u32[]{:S(2)}) %copy-start.2) | copy-done | bytes 7340056
  231.2 3.9 %all-to-all-start.1 = ((f32[2,2,512,384]{3,2,1,0:T(8,128)}), f32[2,2,512,384]{3,2,1,0:T(8,128)S(1)}, u32[]{:S(2)}, u32[]{:S(2)}) async-start(f32[2,2,512,384]{3,2,1,0:T(8,128)} %copy.113), calls=%async_computation.1 | async-start | bytes 6291456 | tf_op jit(solution)/shard_map/all_to_all | solution.py:25
  235.3 2.2 slice-done
  238.2 25.0 %all-to-all-done.1 = f32[2,2,512,384]{3,2,1,0:T(8,128)S(1)} async-done(((f32[2,2,512,384]{3,2,1,0:T(8,128)}), f32[2,2,512,384]{3,2,1,0:T(8,128)S(1)}, u32[]{:S(2)}, u32[]{:S(2)}) %all-to-all-start.1) | async-done | bytes 3145760 | tf_op jit(solution)/shard_map/all_to_all | solution.py:25
  (59 shorter events, 25.8 us)
Async XLA Ops:
  7.2 79.9 %all-gather.3.cloned.1.call-start = ((), (), s32[]{:S(2)}) async-start(), calls=%async_computation.2 | async-start | bytes 2228224 | tf_op jit(solution)/shard_map/all_gather | solution.py:84
  7.9 170.9 %all-gather.5.cloned.1.call-start = ((), (), s32[]{:S(2)}) async-start(), calls=%async_computation.3 | async-start | bytes 4456448 | tf_op jit(solution)/shard_map/all_gather | solution.py:90
  7.9 15.8 %collective-permute-start = (f32[2,64,1024]{2,1,0:T(8,128)}, f32[2,64,1024]{2,1,0:T(8,128)S(1)}, u32[]{:S(2)}, u32[]{:S(2)}) collective-permute-start(f32[2,64,1024]{2,1,0:T(8,128)} %bitcast.121), channel_id=1, source_target_pairs={{0,16},{16,0},{1,17},{17,1},{2,18},{18,2},{3,19},{19,3},{4,20},{20... | collective-permute-start | bytes 1572872 | tf_op jit(solution)/shard_map/ppermute | solution.py:14
  87.1 4.8 %copy-start.3 = (f32[1,2,512,512]{2,3,1,0:T(8,128)S(1)}, f32[1,2,512,512]{2,3,1,0:T(8,128)}, u32[]{:S(2)}) copy-start(f32[1,2,512,512]{2,3,1,0:T(8,128)} %all-gather.3.cloned.1.call-done) | copy-start | bytes 6291460
  91.9 3.0 %copy-start.5 = (f32[1,2,64,1024]{3,2,1,0:T(8,128)S(1)}, f32[1,2,64,1024]{3,2,1,0:T(8,128)}, u32[]{:S(2)}) copy-start(f32[1,2,64,1024]{3,2,1,0:T(8,128)} %param.4) | copy-start | bytes 1572868
  95.0 10.5 %copy-start.6 = (s32[2,8]{1,0:T(2,128)S(1)}, s32[2,8]{1,0:T(2,128)}, u32[]{:S(2)}) copy-start(s32[2,8]{1,0:T(2,128)} %param.7) | copy-start | bytes 196
  97.5 32.6 %all-to-all-start = ((f32[16,1,8192]{2,1,0:T(1,128)}), f32[16,1,8192]{2,1,0:T(1,128)S(1)}, u32[]{:S(2)}, u32[]{:S(2)}) async-start(f32[16,1,8192]{2,1,0:T(1,128)} %reshape.137), calls=%async_computation | async-start | bytes 1048576 | tf_op jit(solution)/shard_map/all_to_all | solution.py:86
  178.8 7.6 %copy-start = (f32[2,1024,512]{2,1,0:T(8,128)S(1)}, f32[2,1024,512]{2,1,0:T(8,128)}, u32[]{:S(2)}) copy-start(f32[2,1024,512]{2,1,0:T(8,128)} %all-gather.5.cloned.1.call-done) | copy-start | bytes 12582916
  188.6 3.5 %copy-start.4 = (f32[2,512,320]{1,2,0:T(8,128)S(1)}, f32[2,512,320]{1,2,0:T(8,128)}, u32[]{:S(2)}) copy-start(f32[2,512,320]{1,2,0:T(8,128)} %param.6) | copy-start | bytes 3932164
  192.1 8.3 %copy-start.1 = (f32[2,1024,512]{2,1,0:T(8,128)S(1)}, f32[2,1024,512]{2,1,0:T(8,128)}, u32[]{:S(2)}) copy-start(f32[2,1024,512]{2,1,0:T(8,128)} %all-gather.5.cloned.1.call-done) | copy-start | bytes 12582916
  226.1 2.9 %copy-start.2 = (f32[2,1024,896]{2,1,0:T(8,128)}, f32[2,1024,896]{2,1,0:T(8,128)S(1)}, u32[]{:S(2)}) copy-start(f32[2,1024,896]{2,1,0:T(8,128)S(1)} %bitcast_select_fusion) | copy-start | bytes 22020100
  231.2 32.0 %all-to-all-start.1 = ((f32[2,2,512,384]{3,2,1,0:T(8,128)}), f32[2,2,512,384]{3,2,1,0:T(8,128)S(1)}, u32[]{:S(2)}, u32[]{:S(2)}) async-start(f32[2,2,512,384]{3,2,1,0:T(8,128)} %copy.113), calls=%async_computation.1 | async-start | bytes 6291456 | tf_op jit(solution)/shard_map/all_to_all | solution.py:25
  235.3 2.2 slice-start
Sparse Core Ops, SparseCore 0:
  10.1 76.9 all-gather.2
  95.0 83.6 all-gather.4
where the time goes:
time: 278 us; the launch traced here: 277 us
  waiting for transfers between devices  168 us (60%)
  local copies, waits for them, and re-layouts  32.3 us (12%)
  matrix products  32 us (12%)
  starting transfers between devices  15.5 us (6%)
  between operations  14.4 us (5%)
  other arithmetic  14.3 us (5%)
    all_gather x1, waiting for transfers between devices, per_device(): lax.all_gather(pivot_inverses, 'grp', axis=3, tiled=True)[0]  62.4 us
    all_gather x1, waiting for transfers between devices, per_device(): piece = lax.all_gather(raw_multipliers, 'grp', axis=1, tiled=True)  43.9 us
    dot_general x12, matrix products, product(): jnp.dot(first_part, second_part, precision=lax.Precision.HIGHEST, preferr...  32 us
    all_to_all x1, waiting for transfers between devices, summed_on_arrival(): lax.all_to_all(pieces, axis, split_axis=0, concat_axis=0, tiled=True)  25 us
    all_to_all x1, waiting for transfers between devices, per_device(): lax.all_to_all(beta_rows, 'grp', split_axis=2, concat_axis=1, tiled=True)  24.2 us
    ppermute x1, waiting for transfers between devices, partner(): return lax.ppermute(block, axis, route)  12.3 us
    gather x4, local copies, waits for them, and re-layouts, reorder(): return jnp.take(grouped, source, axis=1).reshape(matrix.shape)  11.5 us
    unnamed x18, local copies, waits for them, and re-layouts  8.03 us
  transfers between devices with their start and end apart: 5, of which 5 were waited for; matrix products, arithmetic and copies ran while one was open for 3% of the time, Pallas kernels for 0%

commit v1 on v0

v1 whole, which is shorter than its diff:
```python
import functools

import jax
import jax.numpy as jnp
from jax import lax
from jax.experimental import pallas as pl
from jax.experimental.pallas import tpu as pltpu
from jax.sharding import PartitionSpec as P

F32, BF16 = jnp.float32, jnp.bfloat16
NN = (((1,), (0,)), ((), ()))
NT = (((1,), (1,)), ((), ()))
R, L = 0, 1
N = 16
H = N // 2
BLOCKS = 8


def split(x):
    high = x.astype(BF16)
    return high, (x - high.astype(F32)).astype(BF16)


def dot3(a, b, dims):
    d = functools.partial(lax.dot_general, dimension_numbers=dims, preferred_element_type=F32)
    return d(a[0], b[0]) + d(a[0], b[1]) + d(a[1], b[0])


def kernel(
    tab, pt_ref, et_ref, maps_ref,
    schur_ref, ext_ref, mult_ref,
    pt_all, al_all, pack, beta, vh, vl, ph, plo, th, tl, ubuf, sbuf, rbuf,
    pss, prs, ass, ars, bss, brs, yss, yrs, uss, urs,
):
    s = lax.axis_index("sib")
    g = lax.axis_index("grp")
    other = 1 - s
    width = pt_ref.shape[2]
    fx = et_ref.shape[1]
    cols = 64
    e2 = 2 * fx
    rows = e2 + 2 * cols

    def near(d):
        return lax.rem(g + d + N, N)

    pt_all[g] = pt_ref[...]
    al_all[g] = maps_ref[:, :, 0:width]
    lane = lax.broadcasted_iota(jnp.int32, (64, 128), 1)
    for t in range(H):
        re = maps_ref[0, :, t * 128 : (t + 1) * 128]
        im = maps_ref[1, :, t * 128 : (t + 1) * 128]
        pack[2 * t] = jnp.where(lane < 64, re, pltpu.roll(im, 64, 1))
        pack[2 * t + 1] = jnp.where(lane < 64, pltpu.roll(re, 64, 1), im)

    barrier = pltpu.get_barrier_semaphore()
    for d in range(1, N):
        pl.semaphore_signal(barrier, inc=1, device_id={"grp": near(d)}, device_id_type=pl.DeviceIdType.MESH)
    pl.semaphore_signal(barrier, inc=1, device_id={"sib": other}, device_id_type=pl.DeviceIdType.MESH)
    pl.semaphore_wait(barrier, N)

    def hop(buf, ss, rs, way, k, c, arriving):
        back = k if arriving else k - 1
        shard = near(-back if way == R else back)
        return pltpu.make_async_remote_copy(
            src_ref=buf.at[shard, c], dst_ref=buf.at[shard, c],
            send_sem=ss.at[way, c, k - 1], recv_sem=rs.at[way, c, k - 1],
            device_id={"grp": near(1 if way == R else -1)}, device_id_type=pl.DeviceIdType.MESH,
        )

    def parts(k):
        for c in range(2):
            for way in (R, L):
                if k < H or way == c:
                    yield way, c

    pivot = (pt_all, pss, prs)
    alpha = (al_all, ass, ars)

    def start(ring, k):
        for way, c in parts(k):
            hop(*ring, way, k, c, False).start()

    def forward(ring, k):
        onward = tuple(parts(k))
        for way, c in parts(k - 1):
            hop(*ring, way, k - 1, c, True).wait_recv()
            if (way, c) in onward:
                hop(*ring, way, k, c, False).start()

    def arrive(ring, k):
        for way, c in parts(k):
            hop(*ring, way, k, c, True).wait_recv()

    def to_sibling(src, dst, i):
        return pltpu.make_async_remote_copy(
            src_ref=src, dst_ref=dst, send_sem=yss.at[i], recv_sem=yrs.at[i],
            device_id={"sib": other}, device_id_type=pl.DeviceIdType.MESH,
        )

    start(pivot, 1)
    alpha_over = to_sibling(maps_ref.at[:, :, pl.ds(width, width)], al_all.at[g], 0)
    beta_over = to_sibling(pack.at[:, pl.ds(0, 32), :], pack.at[:, pl.ds(0, 32), :], 1)

    @pl.when(s == 0)
    def _():
        alpha_over.start()

    @pl.when(s == 1)
    def _():
        beta_over.start()

    def prepare(c, _):
        high, low = split(et_ref[c])
        vh[pl.ds(pl.multiple_of(c * fx, 16), fx), :] = high
        vl[pl.ds(pl.multiple_of(c * fx, 16), fx), :] = low
        return 0

    lax.fori_loop(0, 2, prepare, 0)

    @pl.when(s == 0)
    def _():
        beta_over.wait_recv()

    @pl.when(s == 1)
    def _():
        alpha_over.wait_recv()

    start(alpha, 1)
    half = pl.ds(pl.multiple_of(s * 32, 32), 32)

    def push(d, arriving):
        to, source = (near(d), g) if not arriving else (g, near(-d))
        return pltpu.make_async_remote_copy(
            src_ref=pack.at[to, half, :], dst_ref=beta.at[source, half, :],
            send_sem=bss.at[d], recv_sem=brs.at[d],
            device_id={"grp": near(d)}, device_id_type=pl.DeviceIdType.MESH,
        )

    for d in range(1, N):
        push(d, False).start()
    beta[g, half, :] = pack[g, half, :]

    for ring, k in (
        (pivot, 2), (pivot, 3), (alpha, 2), (pivot, 4), (pivot, 5), (alpha, 3), (pivot, 6), (pivot, 7), (alpha, 4), (pivot, 8),
    ):
        forward(ring, k)
        if ring is pivot and k == 5:
            for d in range(1, N):
                push(d, True).wait_recv()
            to_sibling(beta.at[:, half, :], beta.at[:, half, :], 2).start()
    forward(alpha, 5)
    other_half = pl.ds(pl.multiple_of(other * 32, 32), 32)
    to_sibling(beta.at[:, other_half, :], beta.at[:, other_half, :], 2).wait_recv()
    for b in range(4):
        block = tab[9 + b]
        both = jnp.concatenate([beta[2 * block], beta[2 * block + 1]], axis=0).T
        high, low = split(both)
        vh[e2:rows, b * 128 : (b + 1) * 128] = high
        vl[e2:rows, b * 128 : (b + 1) * 128] = low
    arrive(pivot, H)

    for c in range(2):
        def widen(j, _, c=c):
            high, low = split(pt_all[j, c])
            at = pl.ds(pl.multiple_of(j * 32, 32), 32)
            ph[c, at, :] = high
            plo[c, at, :] = low
            return 0

        lax.fori_loop(0, N, widen, 0)

    def combine(z):
        a, b = z[:, 0:128], z[:, 128:256]
        return jnp.concatenate(
            [
                a[0:fx] - b[fx:e2], a[fx:e2] + b[0:fx],
                a[e2 : e2 + cols] - b[e2 + cols : rows], a[e2 + cols : rows] + b[e2 : e2 + cols],
            ],
            axis=0,
        )

    def form(q, _):
        at = pl.ds(pl.multiple_of(q * 128, 128), 128)
        right = tuple(jnp.concatenate([p[0, :, at], p[1, :, at]], axis=1) for p in (ph, plo))
        high, low = split(combine(dot3((vh[...], vl[...]), right, NN)))
        th[:, at] = high
        tl[:, at] = low
        return 0

    lax.fori_loop(0, width // 128, form, 0)

    first = lax.div(g, 2)
    sign = 1 - 2 * lax.rem(g, 2)

    def partial(i):
        block = lax.rem(first + sign * lax.div(i + 1, 2) * (1 - 2 * lax.rem(i, 2)) + BLOCKS, BLOCKS)
        right = split(
            jnp.concatenate(
                [al_all[2 * block, 0], al_all[2 * block + 1, 0], al_all[2 * block, 1], al_all[2 * block + 1, 1]], axis=0
            )
        )
        ubuf[block] = combine(dot3((th[...], tl[...]), right, NT))

    def early(i, _):
        partial(i)
        return 0

    lax.fori_loop(0, 4, early, 0)

    def slot(q):
        return pltpu.make_async_remote_copy(
            src_ref=sbuf.at[q], dst_ref=rbuf.at[q], send_sem=uss.at[q], recv_sem=urs.at[q],
            device_id={"sib": other}, device_id_type=pl.DeviceIdType.MESH,
        )

    for q in range(4):
        if q < 3:
            forward(alpha, 6 + q)
        else:
            arrive(alpha, H)
        partial(jnp.int32(4 + q))
        sbuf[q] = ubuf[tab[q]]
        slot(q).start()

    mine = tab[8]
    left = split(jnp.concatenate([al_all[mine, 0], al_all[mine, 1]], axis=0))
    zr = dot3(left, (ph[0], plo[0]), NT)
    zi = dot3(left, (ph[1], plo[1]), NT)
    mult_ref[0] = zr[0:64] - zi[64:128]
    mult_ref[1] = zi[0:64] + zr[64:128]

    for q in range(4):
        slot(q).wait_recv()
    row = lax.broadcasted_iota(jnp.int32, (cols, 128), 1) + s * 512
    col = lax.broadcasted_iota(jnp.int32, (cols, 128), 0) + g * cols
    for p in range(4):
        at = slice(p * 128, (p + 1) * 128)
        total = ubuf[tab[4 + p]] + rbuf[tab[13 + p]]
        ext_ref[0, :, at] = total[0:fx]
        ext_ref[1, :, at] = total[fx:e2]
        one = jnp.where(row + p * 128 == col, 1.0, 0.0).astype(F32)
        schur_ref[0, :, at] = one - total[e2 : e2 + cols]
        schur_ref[1, :, at] = -total[e2 + cols : rows]

    for ring in (pivot, alpha):
        for k in range(1, H + 1):
            for way, c in parts(k):
                hop(*ring, way, k, c, False).wait_send()
    for d in range(1, N):
        push(d, False).wait_send()

    @pl.when(s == 0)
    def _():
        alpha_over.wait_send()

    @pl.when(s == 1)
    def _():
        beta_over.wait_send()

    to_sibling(beta.at[:, half, :], beta.at[:, half, :], 2).wait_send()
    for q in range(4):
        slot(q).wait_send()


def tables(face_blocks, s, g):
    alpha_order, beta_order = face_blocks[0], face_blocks[1]
    slots = jnp.arange(BLOCKS, dtype=jnp.int32)
    alpha_match = (alpha_order[:, None] == slots[None, :]).astype(jnp.int32)
    beta_match = (beta_order[:, None] == slots[None, :]).astype(jnp.int32)
    to_beta = jnp.sum(beta_match * alpha_order[:, None], axis=0)
    to_alpha = jnp.sum(alpha_match * beta_order[:, None], axis=0)
    i = jnp.arange(BLOCKS, dtype=jnp.int32)
    order = (g // 2 + (1 - 2 * (g % 2)) * ((i + 1) // 2) * (1 - 2 * (i % 2)) + BLOCKS) % BLOCKS
    pick = (order[:, None] == slots[None, :]).astype(jnp.int32)
    dest = jnp.sum(pick * to_alpha[None, :], axis=1) // 4
    before = (i[:, None] > i[None, :]).astype(jnp.int32)
    leaves = (dest != s).astype(jnp.int32)
    rank_out = jnp.sum(before * leaves[None, :], axis=1)
    rank_in = jnp.sum(before * (1 - leaves)[None, :], axis=1)
    four = jnp.arange(4, dtype=jnp.int32)
    send = jnp.sum((rank_out[None, :] == four[:, None]) * leaves[None, :] * order[None, :], axis=1)
    own = lax.dynamic_slice_in_dim(to_beta, 4 * s, 4)
    arrives = jnp.sum((order[None, :] == own[:, None]) * rank_in[None, :], axis=1)
    mine = 2 * lax.dynamic_slice_in_dim(to_beta, g // 2, 1) + g % 2
    beta_blocks = lax.dynamic_slice_in_dim(to_alpha, 4 * s, 4)
    return jnp.concatenate([send, own, mine, beta_blocks, arrives]).astype(jnp.int32)


def per_device(interface_maps, pivot_inverses, exterior_coupling, face_blocks):
    s, g = lax.axis_index("sib"), lax.axis_index("grp")
    maps = interface_maps[0]
    pt = jnp.swapaxes(pivot_inverses[0], 1, 2)
    et = jnp.swapaxes(exterior_coupling, 1, 2)
    width, fx = pt.shape[2], et.shape[1]
    rows = 2 * fx + 128
    vmem = pl.BlockSpec(memory_space=pltpu.VMEM)
    dma = pltpu.SemaphoreType.DMA
    schur, ext, mult = pl.pallas_call(
        kernel,
        out_shape=(
            jax.ShapeDtypeStruct((2, 64, 512), F32),
            jax.ShapeDtypeStruct((2, fx, 512), F32),
            jax.ShapeDtypeStruct((2, 64, width), F32),
        ),
        in_specs=[pl.BlockSpec(memory_space=pltpu.SMEM)] + [vmem] * 3,
        out_specs=(vmem,) * 3,
        scratch_shapes=[
            pltpu.VMEM((N, 2, 32, width), F32),
            pltpu.VMEM((N, 2, 64, width), F32),
            pltpu.VMEM((N, 64, 128), F32),
            pltpu.VMEM((N, 64, 128), F32),
            pltpu.VMEM((rows, width), BF16),
            pltpu.VMEM((rows, width), BF16),
            pltpu.VMEM((2, width, width), BF16),
            pltpu.VMEM((2, width, width), BF16),
            pltpu.VMEM((rows, width), BF16),
            pltpu.VMEM((rows, width), BF16),
            pltpu.VMEM((BLOCKS, rows, 128), F32),
            pltpu.VMEM((4, rows, 128), F32),
            pltpu.VMEM((4, rows, 128), F32),
            dma((2, 2, H)), dma((2, 2, H)), dma((2, 2, H)), dma((2, 2, H)),
            dma((N,)), dma((N,)), dma((3,)), dma((3,)), dma((4,)), dma((4,)),
        ],
        compiler_params=pltpu.CompilerParams(collective_id=0, has_side_effects=True, vmem_limit_bytes=56 * 2**20),
    )(tables(face_blocks, s, g), pt, et, maps)
    return jnp.swapaxes(schur, 1, 2), jnp.swapaxes(ext, 1, 2), mult


def solution(mesh):
    in_specs = (P("sib", "box", "grp", None), P("sib", "box", None, "grp"), P("box", "sib", "grp"), P("box", None))
    out_specs = (P("box", "sib", "grp"), P("box", "sib", "grp"), P("box", "grp", "sib"))
    return jax.shard_map(per_device, mesh=mesh, in_specs=in_specs, out_specs=out_specs, check_vma=False)
```

time: 278 us -> 131 us (0.47)
  waiting for transfers between devices: 168 us -> 0 us
  Pallas kernels: 0 us -> 122 us
  matrix products: 32 us -> 0 us
  local copies, waits for them, and re-layouts: 32.3 us -> 6.99 us
  starting transfers between devices: 15.5 us -> 0 us
  other arithmetic: 14.3 us -> 0.63 us
  between operations: 14.4 us -> 1.33 us
    pallas_call x0 -> x1, Pallas kernels: none -> 122 us  [per_device(): pl.pallas_call(kernel, out_shape=(jax.ShapeDtypeStruct((2, 64, 512), F32)...]
    all_gather x2 -> x0, waiting for transfers between devices: 106 us -> none  [the longest x1 62.4 us: per_device(): lax.all_gather(pivot_inverses, 'grp', axis=3, tiled=True)[0]]
    all_to_all x2 -> x0, waiting for transfers between devices: 49.2 us -> none  [the longest x1 25 us: summed_on_arrival(): lax.all_to_all(pieces, axis, split_axis=0, concat_axis=0, tiled=True)]
    dot_general x12 -> x0, matrix products: 32 us -> none  [product(): jnp.dot(first_part, second_part, precision=lax.Precision.HIGHEST, preferr...]
    ppermute x1 -> x0, waiting for transfers between devices: 12.3 us -> none  [partner(): return lax.ppermute(block, axis, route)]
    all_to_all x2 -> x0, starting transfers between devices: 11.9 us -> none  [the longest x1 7.98 us: per_device(): lax.all_to_all(beta_rows, 'grp', split_axis=2, concat_axis=1, tiled=True)]
    gather x4 -> x0, local copies, waits for them, and re-layouts: 11.5 us -> none  [reorder(): return jnp.take(grouped, source, axis=1).reshape(matrix.shape)]
    concatenate x1 -> x0, other arithmetic: 5.49 us -> none  [per_device(): jnp.concatenate([piece, -complex_dot(piece, beta_panel), complex_dot(piec...]
  transfers between devices with their start and end apart: 5 -> 0, of which waited for: 5 -> 0; matrix products, arithmetic and copies ran while one was open for 3% -> 0% of each run, Pallas kernels for 0% -> 0%
where the time goes in v1:
time: 131 us
  Pallas kernels  122 us (93%)
  local copies, waits for them, and re-layouts  6.99 us (5%)
  between operations  1.33 us (1%)
    pallas_call x1, Pallas kernels, per_device(): pl.pallas_call(kernel, out_shape=(jax.ShapeDtypeStruct((2, 64, 512), F32)...  122 us
    unnamed x5, local copies, waits for them, and re-layouts  4.89 us

profile of v1, /device:TPU:6, one launch (start us, length us, event | category | flops | bytes accessed | tf_op | source)
XLA Modules:
  0.0 130.6 jit_solution(14484359818520024122)
XLA Ops:
  0.7 0.8 slice_bitcast_fusion.1
  1.4 0.1 select_reduce_fusion.1
  1.5 0.6 dynamic_slice.10
  2.8 0.1 dynamic_slice.9
  2.8 0.1 dynamic_slice.11
  2.9 0.2 select_reduce_fusion.3
  3.1 0.1 select_reduce_fusion
  3.3 0.2 select_reduce_fusion.5
  3.5 0.6 concatenate.3.tab
  4.1 121.6 %shard_map.67 = (f32[2,64,512]{2,1,0:T(8,128)}, f32[2,320,512]{2,1,0:T(8,128)}, f32[2,64,512]{2,1,0:T(8,128)}) custom-call(s32[17]{0:T(128)} %concatenate.3.tab, f32[2,32,512]{2,1,0:T(8,128)} %bitcast.16, f32[2,320,512]{2,1,0:T(8,128)} %bitcast.12, f32[2,64,1024]{2,1,0:T(8,128)} %bitcast.14), custom_call_target="tpu_custom_call" | custom-call | tf_op jit(solution)/shard_map/pallas_call | solution.py:299
  125.7 1.7 %copy.10 = f32[2,512,64]{1,2,0:T(8,128)} copy(f32[2,512,64]{1,2,0:T(8,128)} %bitcast.15) | data formatting | bytes 524288
  127.4 0.0 copy-start
  127.4 2.5 %copy.11 = f32[2,512,320]{1,2,0:T(8,128)} copy(f32[2,512,320]{1,2,0:T(8,128)} %bitcast.13) | data formatting | bytes 2621440
  129.9 0.0 copy-done
  129.9 0.7 copy.12
  (2 shorter events, 0.0 us)
Async XLA Ops:
  127.4 2.5 %copy-start = (f32[2,64,512]{2,1,0:T(8,128)S(1)}, f32[2,64,512]{2,1,0:T(8,128)}, u32[]{:S(2)}) copy-start(f32[2,64,512]{2,1,0:T(8,128)} %get-tuple-element.24) | copy-start | bytes 786436

commit v2 on v1

v2 whole, which is shorter than its diff:
```python
import functools

import jax
import jax.numpy as jnp
from jax import lax
from jax.experimental import pallas as pl
from jax.experimental.pallas import tpu as pltpu
from jax.sharding import PartitionSpec as P

F32, BF16 = jnp.float32, jnp.bfloat16
NN = (((1,), (0,)), ((), ()))
NT = (((1,), (1,)), ((), ()))
MESH = pl.DeviceIdType.MESH
R, L = 0, 1
N = 16
H = N // 2
BLOCKS = 8
COLS = 64


def split(x):
    high = x.astype(BF16)
    return high, (x - high.astype(F32)).astype(BF16)


def dot3(a, b, dims):
    d = functools.partial(lax.dot_general, dimension_numbers=dims, preferred_element_type=F32)
    return d(a[0], b[0]) + d(a[0], b[1]) + d(a[1], b[0])


def combine(z):
    half = z.shape[0] // 2
    a, b = z[:, 0:128], z[:, 128:256]
    return jnp.concatenate([a[0:half] - b[half:], a[half:] + b[0:half]], axis=0)


def look_up(keys, values, key):
    found = jnp.int32(0)
    for k, v in zip(keys, values):
        found = found + jnp.where(k == key, v, 0)
    return found


def tables(faces_ref, s, g, order):
    alpha_order = [faces_ref[0, j] for j in range(BLOCKS)]
    beta_order = [faces_ref[1, j] for j in range(BLOCKS)]
    send = [jnp.int32(0)] * 4
    out, into = jnp.int32(0), jnp.int32(0)
    rank_in = []
    for block in order:
        place = look_up(alpha_order, beta_order, block)
        leaves = jnp.where(place >= 4, 1, 0) != s
        for q in range(4):
            send[q] = send[q] + jnp.where(jnp.logical_and(leaves, out == q), block, 0)
        rank_in.append(jnp.where(leaves, 0, into))
        out = out + jnp.where(leaves, 1, 0)
        into = into + jnp.where(leaves, 0, 1)
    own = [look_up(beta_order, alpha_order, 4 * s + p) for p in range(4)]
    slots = [look_up(order, rank_in, block) for block in own]
    mine = 2 * look_up(beta_order, alpha_order, lax.div(g, 2)) + lax.rem(g, 2)
    panel = [look_up(alpha_order, beta_order, 4 * s + b) for b in range(4)]
    other_panel = [look_up(alpha_order, beta_order, 4 * (1 - s) + b) for b in range(4)]
    return send, own, slots, mine, panel, other_panel


def kernel(
    faces_ref, pt_ref, et_ref, maps_ref,
    ue_out, ub_out, re_out, rb_out, mult_ref, tab_ref,
    pt_all, al_all, pack, beta, bsend, brecv, bfull, vh, vl, bvh, bvl, ph, plo, th, tl, bth, btl, ubuf, bbuf, sbuf, sbeta,
    pss, prs, ass, ars, bss, brs, yss, yrs, uss, urs, oss,
):
    s = lax.axis_index("sib")
    g = lax.axis_index("grp")
    other = 1 - s
    width = pt_ref.shape[2]
    fx = et_ref.shape[1]

    def near(d):
        return lax.rem(g + d + N, N)

    pt_all[g] = pt_ref[...]
    al_all[g] = maps_ref[:, :, 0:width]
    lane = lax.broadcasted_iota(jnp.int32, (64, 128), 1)
    for t in range(H):
        re = maps_ref[0, :, t * 128 : (t + 1) * 128]
        im = maps_ref[1, :, t * 128 : (t + 1) * 128]
        pack[2 * t] = jnp.where(lane < 64, re, pltpu.roll(im, 64, 1))
        pack[2 * t + 1] = jnp.where(lane < 64, pltpu.roll(re, 64, 1), im)

    barrier = pltpu.get_barrier_semaphore()
    for d in range(1, N):
        pl.semaphore_signal(barrier, inc=1, device_id={"grp": near(d)}, device_id_type=MESH)
    pl.semaphore_signal(barrier, inc=1, device_id={"sib": other}, device_id_type=MESH)
    pl.semaphore_wait(barrier, N)

    def hop(buf, ss, rs, way, k, c, arriving):
        back = k if arriving else k - 1
        shard = near(-back if way == R else back)
        return pltpu.make_async_remote_copy(
            src_ref=buf.at[shard, c], dst_ref=buf.at[shard, c],
            send_sem=ss.at[way, c, k - 1], recv_sem=rs.at[way, c, k - 1],
            device_id={"grp": near(1 if way == R else -1)}, device_id_type=MESH,
        )

    def parts(k):
        for c in range(2):
            for way in (R, L):
                if k < H or way == c:
                    yield way, c

    pivot = (pt_all, pss, prs)
    alpha = (al_all, ass, ars)

    def start(ring, k):
        for way, c in parts(k):
            hop(*ring, way, k, c, False).start()

    def forward(ring, k):
        onward = tuple(parts(k))
        for way, c in parts(k - 1):
            hop(*ring, way, k - 1, c, True).wait_recv()
            if (way, c) in onward:
                hop(*ring, way, k, c, False).start()

    def arrive(ring, k):
        for way, c in parts(k):
            hop(*ring, way, k, c, True).wait_recv()

    def to_sibling(src, dst, send_sem, recv_sem):
        return pltpu.make_async_remote_copy(
            src_ref=src, dst_ref=dst, send_sem=send_sem, recv_sem=recv_sem, device_id={"sib": other}, device_id_type=MESH
        )

    start(pivot, 1)
    alpha_over = to_sibling(maps_ref.at[:, :, pl.ds(width, width)], al_all.at[g], yss.at[0], yrs.at[0])
    beta_over = to_sibling(pack.at[:, pl.ds(0, 32), :], pack.at[:, pl.ds(0, 32), :], yss.at[1], yrs.at[1])
    panel_over = to_sibling(bsend, brecv, yss.at[2], yrs.at[2])
    rest_over = to_sibling(sbeta, rb_out, yss.at[3], yrs.at[3])

    @pl.when(s == 0)
    def _():
        alpha_over.start()
        start(alpha, 1)

    @pl.when(s == 1)
    def _():
        beta_over.start()

    def prepare(c, _):
        at = pl.ds(pl.multiple_of(c * fx, 16), fx)
        high, low = split(et_ref[c])
        vh[at, :] = high
        vl[at, :] = low
        return 0

    lax.fori_loop(0, 2, prepare, 0)

    first = lax.div(g, 2)
    sign = 1 - 2 * lax.rem(g, 2)

    def completes(i):
        return lax.rem(first + sign * lax.div(i + 1, 2) * (1 - 2 * lax.rem(i, 2)) + BLOCKS, BLOCKS)

    forward(pivot, 2)
    send, own, slots, mine, panel, other_panel = tables(faces_ref, s, g, [completes(jnp.int32(i)) for i in range(BLOCKS)])
    for p in range(4):
        tab_ref[p] = own[p]
        tab_ref[4 + p] = slots[p]

    @pl.when(s == 0)
    def _():
        beta_over.wait_recv()

    @pl.when(s == 1)
    def _():
        alpha_over.wait_recv()
        start(alpha, 1)

    half = pl.ds(pl.multiple_of(s * 32, 32), 32)

    def push(d, arriving):
        to, source = (near(d), g) if not arriving else (g, near(-d))
        return pltpu.make_async_remote_copy(
            src_ref=pack.at[to, half, :], dst_ref=beta.at[source, half, :],
            send_sem=bss.at[d], recv_sem=brs.at[d],
            device_id={"grp": near(d)}, device_id_type=MESH,
        )

    for ring, k in ((pivot, 3), (pivot, 4), (alpha, 2), (pivot, 5), (pivot, 6), (pivot, 7), (pivot, 8), (alpha, 3)):
        forward(ring, k)
    arrive(pivot, H)

    for c in range(2):
        def widen(j, _, c=c):
            high, low = split(pt_all[j, c])
            at = pl.ds(pl.multiple_of(j * 32, 32), 32)
            ph[c, at, :] = high
            plo[c, at, :] = low
            return 0

        lax.fori_loop(0, N, widen, 0)

    def form(q, left, high_ref, low_ref):
        at = pl.ds(pl.multiple_of(q * 128, 128), 128)
        right = tuple(jnp.concatenate([p[0, :, at], p[1, :, at]], axis=1) for p in (ph, plo))
        high, low = split(combine(dot3(tuple(ref[...] for ref in left), right, NN)))
        high_ref[:, at] = high
        low_ref[:, at] = low

    def form_exterior(q, _):
        form(q, (vh, vl), th, tl)
        return 0

    def form_beta(q, _):
        form(q, (bvh, bvl), bth, btl)
        return 0

    def rows_of(block):
        a, b = al_all.at[2 * block], al_all.at[2 * block + 1]
        return split(jnp.concatenate([a[0], b[0], a[1], b[1]], axis=0))

    def keep(block):
        return pltpu.make_async_copy(ubuf.at[block], ue_out.at[block], oss.at[block])

    def partial(i, _):
        block = completes(i)
        ubuf[block] = combine(dot3((th[...], tl[...]), rows_of(block), NT))
        keep(block).start()
        return 0

    def partial_beta(block, _):
        bbuf[block] = combine(dot3((bth[...], btl[...]), rows_of(block), NT))
        return 0

    def slot(q):
        return to_sibling(sbuf.at[q], re_out.at[q], uss.at[q], urs.at[q])

    def ship(q):
        partial(jnp.int32(4 + q), 0)
        sbuf[q] = ubuf[send[q]]
        slot(q).start()

    lax.fori_loop(0, 2, form_exterior, 0)
    forward(alpha, 4)
    lax.fori_loop(2, 4, form_exterior, 0)
    forward(alpha, 5)
    lax.fori_loop(0, 4, partial, 0)
    forward(alpha, 6)
    ship(0)
    forward(alpha, 7)
    for d in range(1, N):
        push(d, False).start()
    beta[g, half, :] = pack[g, half, :]
    ship(1)
    forward(alpha, 8)
    ship(2)

    for d in range(1, N):
        push(d, True).wait_recv()
    for b in range(4):
        for c in range(2):
            bsend[b, c] = beta[2 * other_panel[b] + c, half, :]
    panel_over.start()
    arrive(alpha, H)
    ship(3)

    panel_over.wait_recv()
    for b in range(4):
        for c in range(2):
            bfull[c, half, :] = beta[2 * panel[b] + c, half, :]
            bfull[c, pl.ds(pl.multiple_of(other * 32, 32), 32), :] = brecv[b, c]
        high, low = split(bfull[...].reshape(128, 128).T)
        bvh[:, b * 128 : (b + 1) * 128] = high
        bvl[:, b * 128 : (b + 1) * 128] = low
    lax.fori_loop(0, 4, form_beta, 0)
    lax.fori_loop(0, BLOCKS, partial_beta, 0)
    for q in range(4):
        sbeta[q] = bbuf[send[q]]
    rest_over.start()
    keep_beta = pltpu.make_async_copy(bbuf, ub_out, oss.at[BLOCKS])
    keep_beta.start()

    left = split(jnp.concatenate([al_all[mine, 0], al_all[mine, 1]], axis=0))
    zr = dot3(left, (ph[0], plo[0]), NT)
    zi = dot3(left, (ph[1], plo[1]), NT)
    mult_ref[0] = zr[0:64] - zi[64:128]
    mult_ref[1] = zi[0:64] + zr[64:128]

    for ring in (pivot, alpha):
        for k in range(1, H + 1):
            for way, c in parts(k):
                hop(*ring, way, k, c, False).wait_send()
    for d in range(1, N):
        push(d, False).wait_send()

    @pl.when(s == 0)
    def _():
        alpha_over.wait_send()

    @pl.when(s == 1)
    def _():
        beta_over.wait_send()

    for block in range(BLOCKS):
        keep(block).wait()
    keep_beta.wait()
    panel_over.wait_send()
    for q in range(4):
        slot(q).wait()
    rest_over.wait()


def place(tab, ue_ref, ub_ref, re_ref, rb_ref, mult_ref, schur_ref, ext_ref, out_ref):
    p = pl.program_id(0)
    fx = ext_ref.shape[1]
    ext_ref[0] = ue_ref[0, 0:fx] + re_ref[0, 0:fx]
    ext_ref[1] = ue_ref[0, fx:] + re_ref[0, fx:]
    row = lax.broadcasted_iota(jnp.int32, (COLS, 128), 1) + (lax.axis_index("sib") * 4 + p) * 128
    col = lax.broadcasted_iota(jnp.int32, (COLS, 128), 0) + lax.axis_index("grp") * COLS
    one = jnp.where(row == col, 1.0, 0.0).astype(F32)
    schur_ref[0] = one - (ub_ref[0, 0:COLS] + rb_ref[0, 0:COLS])
    schur_ref[1] = -(ub_ref[0, COLS:] + rb_ref[0, COLS:])
    out_ref[...] = mult_ref[...]


def per_device(interface_maps, pivot_inverses, exterior_coupling, face_blocks):
    maps = interface_maps[0]
    pt = jnp.swapaxes(pivot_inverses[0], 1, 2)
    et = jnp.swapaxes(exterior_coupling, 1, 2)
    width, fx = pt.shape[2], et.shape[1]
    vmem = pl.BlockSpec(memory_space=pltpu.VMEM)
    smem = pl.BlockSpec(memory_space=pltpu.SMEM)
    hbm = pl.BlockSpec(memory_space=pltpu.HBM)
    dma = pltpu.SemaphoreType.DMA
    ue, ub, re, rb, mult, tab = pl.pallas_call(
        kernel,
        out_shape=(
            jax.ShapeDtypeStruct((BLOCKS, 2 * fx, 128), F32),
            jax.ShapeDtypeStruct((BLOCKS, 2 * COLS, 128), F32),
            jax.ShapeDtypeStruct((4, 2 * fx, 128), F32),
            jax.ShapeDtypeStruct((4, 2 * COLS, 128), F32),
            jax.ShapeDtypeStruct((2, 64, width), F32),
            jax.ShapeDtypeStruct((8,), jnp.int32),
        ),
        in_specs=[smem, vmem, vmem, vmem],
        out_specs=(hbm, hbm, hbm, hbm, vmem, smem),
        scratch_shapes=[
            pltpu.VMEM((N, 2, 32, width), F32),
            pltpu.VMEM((N, 2, 64, width), F32),
            pltpu.VMEM((N, 64, 128), F32),
            pltpu.VMEM((N, 64, 128), F32),
            pltpu.VMEM((4, 2, 32, 128), F32),
            pltpu.VMEM((4, 2, 32, 128), F32),
            pltpu.VMEM((2, 64, 128), F32),
            pltpu.VMEM((2 * fx, width), BF16),
            pltpu.VMEM((2 * fx, width), BF16),
            pltpu.VMEM((2 * COLS, width), BF16),
            pltpu.VMEM((2 * COLS, width), BF16),
            pltpu.VMEM((2, width, width), BF16),
            pltpu.VMEM((2, width, width), BF16),
            pltpu.VMEM((2 * fx, width), BF16),
            pltpu.VMEM((2 * fx, width), BF16),
            pltpu.VMEM((2 * COLS, width), BF16),
            pltpu.VMEM((2 * COLS, width), BF16),
            pltpu.VMEM((BLOCKS, 2 * fx, 128), F32),
            pltpu.VMEM((BLOCKS, 2 * COLS, 128), F32),
            pltpu.VMEM((4, 2 * fx, 128), F32),
            pltpu.VMEM((4, 2 * COLS, 128), F32),
            dma((2, 2, H)), dma((2, 2, H)), dma((2, 2, H)), dma((2, 2, H)),
            dma((N,)), dma((N,)), dma((4,)), dma((4,)), dma((4,)), dma((4,)), dma((BLOCKS + 1,)),
        ],
        compiler_params=pltpu.CompilerParams(collective_id=0, has_side_effects=True, vmem_limit_bytes=56 * 2**20),
    )(face_blocks, pt, et, maps)

    def block(shape, index):
        return pl.BlockSpec(shape, index)

    schur, ext, mult = pl.pallas_call(
        place,
        grid_spec=pltpu.PrefetchScalarGridSpec(
            num_scalar_prefetch=1,
            grid=(4,),
            in_specs=[
                block((1, 2 * fx, 128), lambda p, tab: (tab[p], 0, 0)),
                block((1, 2 * COLS, 128), lambda p, tab: (tab[p], 0, 0)),
                block((1, 2 * fx, 128), lambda p, tab: (tab[4 + p], 0, 0)),
                block((1, 2 * COLS, 128), lambda p, tab: (tab[4 + p], 0, 0)),
                block((2, 64, 128), lambda p, tab: (0, 0, p)),
            ],
            out_specs=[
                block((2, COLS, 128), lambda p, tab: (0, 0, p)),
                block((2, fx, 128), lambda p, tab: (0, 0, p)),
                block((2, 64, 128), lambda p, tab: (0, 0, p)),
            ],
        ),
        out_shape=(
            jax.ShapeDtypeStruct((2, COLS, 512), F32),
            jax.ShapeDtypeStruct((2, fx, 512), F32),
            jax.ShapeDtypeStruct((2, 64, width), F32),
        ),
    )(tab, ue, ub, re, rb, mult)
    return jnp.swapaxes(schur, 1, 2), jnp.swapaxes(ext, 1, 2), mult


def solution(mesh):
    in_specs = (P("sib", "box", "grp", None), P("sib", "box", None, "grp"), P("box", "sib", "grp"), P("box", None))
    out_specs = (P("box", "sib", "grp"), P("box", "sib", "grp"), P("box", "grp", "sib"))
    return jax.shard_map(per_device, mesh=mesh, in_specs=in_specs, out_specs=out_specs, check_vma=False)
```

time: 131 us -> 122 us (0.931)
  local copies, waits for them, and re-layouts: 6.99 us -> 0 us
    unnamed x5 -> x0, local copies, waits for them, and re-layouts: 4.89 us -> none
    pallas_call x1 -> x2, Pallas kernels: 122 us -> 121 us  [the longest x1 117 us: per_device(): pl.pallas_call(kernel, out_shape=(jax.ShapeDtypeStruct((BLOCKS, 2 * fx, 1...]
where the time goes in v2:
time: 122 us
  Pallas kernels  121 us (99%)
    pallas_call x1, Pallas kernels, per_device(): pl.pallas_call(kernel, out_shape=(jax.ShapeDtypeStruct((BLOCKS, 2 * fx, 1...  117 us
    pallas_call x1, Pallas kernels, per_device(): pl.pallas_call(place, grid_spec=pltpu.PrefetchScalarGridSpec(num_scalar_p...  4.62 us

profile of v2, /device:TPU:6, one launch (start us, length us, event | category | flops | bytes accessed | tf_op | source)
XLA Modules:
  0.0 122.0 jit_solution(11982597042088617539)
XLA Ops:
  0.6 116.7 %shard_map.67 = (f32[8,640,128]{2,1,0:T(8,128)}, f32[8,128,128]{2,1,0:T(8,128)}, f32[4,640,128]{2,1,0:T(8,128)}, f32[4,128,128]{2,1,0:T(8,128)}, f32[2,64,512]{2,1,0:T(8,128)}, /*index=5*/s32[8]{0:T(128)}) custom-call(s32[2,8]{1,0:T(2,128)} %faces_ref.1, f32[2,32,512]{2,1,0:T(8,128)} %bitcast.9, f32[2,320,512]{2,1,0:T(8,128)} %bitcast.7, f32[2,64,1024]{2,1,0:T(8,128)} %bitcast.8), custom_call_target="tpu_custom_call" | custom-call | tf_op jit(solution)/shard_map/pallas_call | solution.py:335
  117.4 4.6 %shard_map.68 = (f32[2,64,512]{2,1,0:T(8,128)}, f32[2,320,512]{2,1,0:T(8,128)}, f32[2,64,512]{2,1,0:T(8,128)}) custom-call(s32[8]{0:T(128)} %get-tuple-element.12.tab, f32[8,640,128]{2,1,0:T(8,128)} %get-tuple-element.13.ue_ref, f32[8,128,128]{2,1,0:T(8,128)} %get-tuple-element.14.ub_ref, f32[4,640,128]{2,1,0:T(8,128)} %get-tuple-element.15.re_ref, ...), custom_call_target="tpu_custom_call" | custom-call | tf_op jit(solution)/shard_map/pallas_call | solution.py:378

commit v3 on v2

--- a/solution.py
+++ b/solution.py
@@ -66,32 +66,42 @@
 def kernel(
     faces_ref, pt_ref, et_ref, maps_ref,
     ue_out, ub_out, re_out, rb_out, mult_ref, tab_ref,
-    pt_all, al_all, pack, beta, bsend, brecv, bfull, vh, vl, bvh, bvl, ph, plo, th, tl, bth, btl, ubuf, bbuf, sbuf, sbeta,
-    pss, prs, ass, ars, bss, brs, yss, yrs, uss, urs, oss,
+    pt_all, al_all, pack, held, et_in, beta, bsend, brecv, bfull, vh, vl, bvh, bvl, ph, plo, th, tl, bth, btl, ubuf, bbuf, sbuf, sbeta,
+    pss, prs, ass, ars, bss, brs, yss, yrs, uss, urs, oss, ess,
 ):
     s = lax.axis_index("sib")
     g = lax.axis_index("grp")
     other = 1 - s
     width = pt_ref.shape[2]
     fx = et_ref.shape[1]
+    width2 = pl.ds(width, width)
 
     def near(d):
         return lax.rem(g + d + N, N)
 
+    barrier = pltpu.get_barrier_semaphore()
+    for peer in ({"grp": near(1)}, {"grp": near(-1)}, {"sib": other}):
+        pl.semaphore_signal(barrier, inc=1, device_id=peer, device_id_type=MESH)
+    fetch = pltpu.make_async_copy(et_ref, et_in, ess)
+    fetch.start()
+
     pt_all[g] = pt_ref[...]
-    al_all[g] = maps_ref[:, :, 0:width]
-    lane = lax.broadcasted_iota(jnp.int32, (64, 128), 1)
-    for t in range(H):
-        re = maps_ref[0, :, t * 128 : (t + 1) * 128]
-        im = maps_ref[1, :, t * 128 : (t + 1) * 128]
-        pack[2 * t] = jnp.where(lane < 64, re, pltpu.roll(im, 64, 1))
-        pack[2 * t + 1] = jnp.where(lane < 64, pltpu.roll(re, 64, 1), im)
-
-    barrier = pltpu.get_barrier_semaphore()
-    for d in range(1, N):
-        pl.semaphore_signal(barrier, inc=1, device_id={"grp": near(d)}, device_id_type=MESH)
-    pl.semaphore_signal(barrier, inc=1, device_id={"sib": other}, device_id_type=MESH)
-    pl.semaphore_wait(barrier, N)
+
+    @pl.when(s == 0)
+    def _():
+        al_all[g] = maps_ref[:, :, 0:width]
+
+    @pl.when(s == 1)
+    def _():
+        lane = lax.broadcasted_iota(jnp.int32, (32, 128), 1)
+        for ref, at in ((pack, 0), (held, 32)):
+            for t in range(H):
+                re = maps_ref[0, at : at + 32, t * 128 : (t + 1) * 128]
+                im = maps_ref[1, at : at + 32, t * 128 : (t + 1) * 128]
+                ref[2 * t] = jnp.where(lane < 64, re, pltpu.roll(im, 64, 1))
+                ref[2 * t + 1] = jnp.where(lane < 64, pltpu.roll(re, 64, 1), im)
+
+    pl.semaphore_wait(barrier, 3)
 
     def hop(buf, ss, rs, way, k, c, arriving):
         back = k if arriving else k - 1
@@ -132,23 +142,35 @@
         )
 
     start(pivot, 1)
-    alpha_over = to_sibling(maps_ref.at[:, :, pl.ds(width, width)], al_all.at[g], yss.at[0], yrs.at[0])
-    beta_over = to_sibling(pack.at[:, pl.ds(0, 32), :], pack.at[:, pl.ds(0, 32), :], yss.at[1], yrs.at[1])
+    alpha_over = [to_sibling(maps_ref.at[c, :, width2], al_all.at[g, c], yss.at[4 + c], yrs.at[4 + c]) for c in range(2)]
+    beta_over = to_sibling(pack, held, yss.at[1], yrs.at[1])
     panel_over = to_sibling(bsend, brecv, yss.at[2], yrs.at[2])
     rest_over = to_sibling(sbeta, rb_out, yss.at[3], yrs.at[3])
 
     @pl.when(s == 0)
     def _():
-        alpha_over.start()
+        for copy in alpha_over:
+            copy.start()
         start(alpha, 1)
 
     @pl.when(s == 1)
     def _():
         beta_over.start()
+
+    forward(pivot, 2)
+
+    @pl.when(s == 1)
+    def _():
+        for c in range(2):
+            alpha_over[c].wait_recv()
+            for way in (R, L):
+                hop(*alpha, way, 1, c, False).start()
+
+    fetch.wait()
 
     def prepare(c, _):
         at = pl.ds(pl.multiple_of(c * fx, 16), fx)
-        high, low = split(et_ref[c])
+        high, low = split(et_in[c])
         vh[at, :] = high
         vl[at, :] = low
         return 0
@@ -161,32 +183,23 @@
     def completes(i):
         return lax.rem(first + sign * lax.div(i + 1, 2) * (1 - 2 * lax.rem(i, 2)) + BLOCKS, BLOCKS)
 
-    forward(pivot, 2)
+    forward(pivot, 3)
     send, own, slots, mine, panel, other_panel = tables(faces_ref, s, g, [completes(jnp.int32(i)) for i in range(BLOCKS)])
     for p in range(4):
         tab_ref[p] = own[p]
         tab_ref[4 + p] = slots[p]
 
-    @pl.when(s == 0)
-    def _():
-        beta_over.wait_recv()
-
-    @pl.when(s == 1)
-    def _():
-        alpha_over.wait_recv()
-        start(alpha, 1)
-
     half = pl.ds(pl.multiple_of(s * 32, 32), 32)
 
     def push(d, arriving):
         to, source = (near(d), g) if not arriving else (g, near(-d))
         return pltpu.make_async_remote_copy(
-            src_ref=pack.at[to, half, :], dst_ref=beta.at[source, half, :],
+            src_ref=held.at[to], dst_ref=beta.at[source, half, :],
             send_sem=bss.at[d], recv_sem=brs.at[d],
             device_id={"grp": near(d)}, device_id_type=MESH,
         )
 
-    for ring, k in ((pivot, 3), (pivot, 4), (alpha, 2), (pivot, 5), (pivot, 6), (pivot, 7), (pivot, 8), (alpha, 3)):
+    for ring, k in ((pivot, 4), (alpha, 2), (pivot, 5), (pivot, 6), (alpha, 3), (pivot, 7), (pivot, 8), (alpha, 4)):
         forward(ring, k)
     arrive(pivot, H)
 
@@ -240,17 +253,20 @@
         sbuf[q] = ubuf[send[q]]
         slot(q).start()
 
-    lax.fori_loop(0, 2, form_exterior, 0)
-    forward(alpha, 4)
-    lax.fori_loop(2, 4, form_exterior, 0)
+    lax.fori_loop(0, 4, form_exterior, 0)
     forward(alpha, 5)
     lax.fori_loop(0, 4, partial, 0)
     forward(alpha, 6)
     ship(0)
     forward(alpha, 7)
+
+    @pl.when(s == 0)
+    def _():
+        beta_over.wait_recv()
+
     for d in range(1, N):
         push(d, False).start()
-    beta[g, half, :] = pack[g, half, :]
+    beta[g, half, :] = held[g]
     ship(1)
     forward(alpha, 8)
     ship(2)
@@ -295,7 +311,8 @@
 
     @pl.when(s == 0)
     def _():
-        alpha_over.wait_send()
+        for copy in alpha_over:
+            copy.wait_send()
 
     @pl.when(s == 1)
     def _():
@@ -310,17 +327,36 @@
     rest_over.wait()
 
 
-def place(tab, ue_ref, ub_ref, re_ref, rb_ref, mult_ref, schur_ref, ext_ref, out_ref):
-    p = pl.program_id(0)
+def place(tab, ue_ref, ub_ref, re_ref, rb_ref, mult_ref, schur_ref, ext_ref, out_ref, ue, ub, re, rb, mult, schur, ext, sems):
     fx = ext_ref.shape[1]
-    ext_ref[0] = ue_ref[0, 0:fx] + re_ref[0, 0:fx]
-    ext_ref[1] = ue_ref[0, fx:] + re_ref[0, fx:]
-    row = lax.broadcasted_iota(jnp.int32, (COLS, 128), 1) + (lax.axis_index("sib") * 4 + p) * 128
+    through = pltpu.make_async_copy(mult_ref, mult, sems.at[0, 8])
+    through.start()
+    reads, writes = [], []
+    for p in range(4):
+        own, slot = tab[p], tab[4 + p]
+        pairs = ((ue_ref.at[own], ue.at[p]), (re_ref.at[slot], re.at[p]), (ub_ref.at[own], ub.at[p]), (rb_ref.at[slot], rb.at[p]))
+        reads.append([pltpu.make_async_copy(a, b, sems.at[p, i]) for i, (a, b) in enumerate(pairs)])
+        for copy in reads[p]:
+            copy.start()
     col = lax.broadcasted_iota(jnp.int32, (COLS, 128), 0) + lax.axis_index("grp") * COLS
-    one = jnp.where(row == col, 1.0, 0.0).astype(F32)
-    schur_ref[0] = one - (ub_ref[0, 0:COLS] + rb_ref[0, 0:COLS])
-    schur_ref[1] = -(ub_ref[0, COLS:] + rb_ref[0, COLS:])
-    out_ref[...] = mult_ref[...]
+    row = lax.broadcasted_iota(jnp.int32, (COLS, 128), 1) + lax.axis_index("sib") * 512
+    for p in range(4):
+        at = slice(p * 128, (p + 1) * 128)
+        for copy in reads[p]:
+            copy.wait()
+        ext[0, :, at] = ue[p, 0:fx] + re[p, 0:fx]
+        ext[1, :, at] = ue[p, fx:] + re[p, fx:]
+        one = jnp.where(row + p * 128 == col, 1.0, 0.0).astype(F32)
+        schur[0, :, at] = one - (ub[p, 0:COLS] + rb[p, 0:COLS])
+        schur[1, :, at] = -(ub[p, COLS:] + rb[p, COLS:])
+        for i, (a, b) in enumerate(((ext, ext_ref), (schur, schur_ref))):
+            writes.append(pltpu.make_async_copy(a.at[:, :, at], b.at[:, :, at], sems.at[p, 4 + i]))
+            writes[-1].start()
+    through.wait()
+    writes.append(pltpu.make_async_copy(mult, out_ref, sems.at[1, 8]))
+    writes[-1].start()
+    for copy in writes:
+        copy.wait()
 
 
 def per_device(interface_maps, pivot_inverses, exterior_coupling, face_blocks):
@@ -342,12 +378,14 @@
             jax.ShapeDtypeStruct((2, 64, width), F32),
             jax.ShapeDtypeStruct((8,), jnp.int32),
         ),
-        in_specs=[smem, vmem, vmem, vmem],
+        in_specs=[smem, vmem, hbm, vmem],
         out_specs=(hbm, hbm, hbm, hbm, vmem, smem),
         scratch_shapes=[
             pltpu.VMEM((N, 2, 32, width), F32),
             pltpu.VMEM((N, 2, 64, width), F32),
-            pltpu.VMEM((N, 64, 128), F32),
+            pltpu.VMEM((N, 32, 128), F32),
+            pltpu.VMEM((N, 32, 128), F32),
+            pltpu.VMEM((2, fx, width), F32),
             pltpu.VMEM((N, 64, 128), F32),
             pltpu.VMEM((4, 2, 32, 128), F32),
             pltpu.VMEM((4, 2, 32, 128), F32),
@@ -367,37 +405,30 @@
             pltpu.VMEM((4, 2 * fx, 128), F32),
             pltpu.VMEM((4, 2 * COLS, 128), F32),
             dma((2, 2, H)), dma((2, 2, H)), dma((2, 2, H)), dma((2, 2, H)),
-            dma((N,)), dma((N,)), dma((4,)), dma((4,)), dma((4,)), dma((4,)), dma((BLOCKS + 1,)),
+            dma((N,)), dma((N,)), dma((6,)), dma((6,)), dma((4,)), dma((4,)), dma((BLOCKS + 1,)), dma,
         ],
         compiler_params=pltpu.CompilerParams(collective_id=0, has_side_effects=True, vmem_limit_bytes=56 * 2**20),
     )(face_blocks, pt, et, maps)
 
-    def block(shape, index):
-        return pl.BlockSpec(shape, index)
-
     schur, ext, mult = pl.pallas_call(
         place,
-        grid_spec=pltpu.PrefetchScalarGridSpec(
-            num_scalar_prefetch=1,
-            grid=(4,),
-            in_specs=[
-                block((1, 2 * fx, 128), lambda p, tab: (tab[p], 0, 0)),
-                block((1, 2 * COLS, 128), lambda p, tab: (tab[p], 0, 0)),
-                block((1, 2 * fx, 128), lambda p, tab: (tab[4 + p], 0, 0)),
-                block((1, 2 * COLS, 128), lambda p, tab: (tab[4 + p], 0, 0)),
-                block((2, 64, 128), lambda p, tab: (0, 0, p)),
-            ],
-            out_specs=[
-                block((2, COLS, 128), lambda p, tab: (0, 0, p)),
-                block((2, fx, 128), lambda p, tab: (0, 0, p)),
-                block((2, 64, 128), lambda p, tab: (0, 0, p)),
-            ],
-        ),
+        in_specs=[smem] + [hbm] * 5,
+        out_specs=(hbm,) * 3,
         out_shape=(
             jax.ShapeDtypeStruct((2, COLS, 512), F32),
             jax.ShapeDtypeStruct((2, fx, 512), F32),
             jax.ShapeDtypeStruct((2, 64, width), F32),
         ),
+        scratch_shapes=[
+            pltpu.VMEM((4, 2 * fx, 128), F32),
+            pltpu.VMEM((4, 2 * COLS, 128), F32),
+            pltpu.VMEM((4, 2 * fx, 128), F32),
+            pltpu.VMEM((4, 2 * COLS, 128), F32),
+            pltpu.VMEM((2, 64, width), F32),
+            pltpu.VMEM((2, COLS, 512), F32),
+            pltpu.VMEM((2, fx, 512), F32),
+            dma((4, 9)),
+        ],
     )(tab, ue, ub, re, rb, mult)
     return jnp.swapaxes(schur, 1, 2), jnp.swapaxes(ext, 1, 2), mult
 

time: 122 us -> 114 us (0.934); the launches traced: 122 us -> 113 us
  Pallas kernels: 121 us -> 112 us
    pallas_call x1, Pallas kernels: 117 us -> 108 us  [per_device(): pl.pallas_call(kernel, out_shape=(jax.ShapeDtypeStruct((BLOCKS, 2 * fx, 1...]
where the time goes in v3:
time: 114 us; the launch traced here: 113 us
  Pallas kernels  112 us (98%)
    pallas_call x1, Pallas kernels, per_device(): pl.pallas_call(kernel, out_shape=(jax.ShapeDtypeStruct((BLOCKS, 2 * fx, 1...  108 us
    pallas_call x1, Pallas kernels, per_device(): pl.pallas_call(place, in_specs=[smem] + [hbm] * 5, out_specs=(hbm,) * 3,...  3.74 us

profile of v3, /device:TPU:6, one launch (start us, length us, event | category | flops | bytes accessed | tf_op | source)
XLA Modules:
  0.0 112.7 jit_solution(4352988742246469608)
XLA Ops:
  0.6 108.3 %shard_map.67 = (f32[8,640,128]{2,1,0:T(8,128)}, f32[8,128,128]{2,1,0:T(8,128)}, f32[4,640,128]{2,1,0:T(8,128)}, f32[4,128,128]{2,1,0:T(8,128)}, f32[2,64,512]{2,1,0:T(8,128)}, /*index=5*/s32[8]{0:T(128)}) custom-call(s32[2,8]{1,0:T(2,128)} %faces_ref.1, f32[2,32,512]{2,1,0:T(8,128)} %bitcast.9, f32[2,320,512]{2,1,0:T(8,128)} %bitcast.7, f32[2,64,1024]{2,1,0:T(8,128)} %bitcast.8), custom_call_target="tpu_custom_call" | custom-call | tf_op jit(solution)/shard_map/pallas_call | solution.py:371
  109.0 3.7 %shard_map.68 = (f32[2,64,512]{2,1,0:T(8,128)}, f32[2,320,512]{2,1,0:T(8,128)}, f32[2,64,512]{2,1,0:T(8,128)}) custom-call(s32[8]{0:T(128)} %get-tuple-element.12.tab, f32[8,640,128]{2,1,0:T(8,128)} %get-tuple-element.13.ue_ref, f32[8,128,128]{2,1,0:T(8,128)} %get-tuple-element.14.ub_ref, f32[4,640,128]{2,1,0:T(8,128)} %get-tuple-element.15.re_ref, ...), custom_call_target="tpu_custom_call" | custom-call | tf_op jit(solution)/shard_map/pallas_call | solution.py:413

commit v4 on v3

--- a/solution.py
+++ b/solution.py
@@ -66,7 +66,7 @@
 def kernel(
     faces_ref, pt_ref, et_ref, maps_ref,
     ue_out, ub_out, re_out, rb_out, mult_ref, tab_ref,
-    pt_all, al_all, pack, held, et_in, beta, bsend, brecv, bfull, vh, vl, bvh, bvl, ph, plo, th, tl, bth, btl, ubuf, bbuf, sbuf, sbeta,
+    pt_all, al_all, pack, held, et_in, maps_in, beta, bsend, brecv, bfull, vh, vl, bvh, bvl, ph, plo, th, tl, bth, btl, ubuf, bbuf, sbuf, sbeta,
     pss, prs, ass, ars, bss, brs, yss, yrs, uss, urs, oss, ess,
 ):
     s = lax.axis_index("sib")
@@ -82,25 +82,35 @@
     barrier = pltpu.get_barrier_semaphore()
     for peer in ({"grp": near(1)}, {"grp": near(-1)}, {"sib": other}):
         pl.semaphore_signal(barrier, inc=1, device_id=peer, device_id_type=MESH)
-    fetch = pltpu.make_async_copy(et_ref, et_in, ess)
+    fetch = pltpu.make_async_copy(et_ref, et_in, ess.at[0])
+    fetch_pivot = pltpu.make_async_copy(pt_ref, pt_all.at[g], ess.at[1])
+    fetch_maps = pltpu.make_async_copy(maps_ref, maps_in, ess.at[2])
+    fetch_alpha = pltpu.make_async_copy(maps_ref.at[:, :, pl.ds(0, width)], al_all.at[g], ess.at[3])
+    fetch_pivot.start()
+    fetch_maps.start()
+
+    @pl.when(s == 0)
+    def _():
+        fetch_alpha.start()
+
     fetch.start()
-
-    pt_all[g] = pt_ref[...]
+    fetch_maps.wait()
 
     @pl.when(s == 0)
     def _():
-        al_all[g] = maps_ref[:, :, 0:width]
+        fetch_alpha.wait()
 
     @pl.when(s == 1)
     def _():
         lane = lax.broadcasted_iota(jnp.int32, (32, 128), 1)
         for ref, at in ((pack, 0), (held, 32)):
             for t in range(H):
-                re = maps_ref[0, at : at + 32, t * 128 : (t + 1) * 128]
-                im = maps_ref[1, at : at + 32, t * 128 : (t + 1) * 128]
+                re = maps_in[0, at : at + 32, t * 128 : (t + 1) * 128]
+                im = maps_in[1, at : at + 32, t * 128 : (t + 1) * 128]
                 ref[2 * t] = jnp.where(lane < 64, re, pltpu.roll(im, 64, 1))
                 ref[2 * t + 1] = jnp.where(lane < 64, pltpu.roll(re, 64, 1), im)
 
+    fetch_pivot.wait()
     pl.semaphore_wait(barrier, 3)
 
     def hop(buf, ss, rs, way, k, c, arriving):
@@ -125,9 +135,11 @@
         for way, c in parts(k):
             hop(*ring, way, k, c, False).start()
 
-    def forward(ring, k):
+    def forward(ring, k, planes=(0, 1)):
         onward = tuple(parts(k))
         for way, c in parts(k - 1):
+            if c not in planes:
+                continue
             hop(*ring, way, k - 1, c, True).wait_recv()
             if (way, c) in onward:
                 hop(*ring, way, k, c, False).start()
@@ -142,7 +154,7 @@
         )
 
     start(pivot, 1)
-    alpha_over = [to_sibling(maps_ref.at[c, :, width2], al_all.at[g, c], yss.at[4 + c], yrs.at[4 + c]) for c in range(2)]
+    alpha_over = [to_sibling(maps_in.at[c, :, width2], al_all.at[g, c], yss.at[4 + c], yrs.at[4 + c]) for c in range(2)]
     beta_over = to_sibling(pack, held, yss.at[1], yrs.at[1])
     panel_over = to_sibling(bsend, brecv, yss.at[2], yrs.at[2])
     rest_over = to_sibling(sbeta, rb_out, yss.at[3], yrs.at[3])
@@ -199,8 +211,10 @@
             device_id={"grp": near(d)}, device_id_type=MESH,
         )
 
-    for ring, k in ((pivot, 4), (alpha, 2), (pivot, 5), (pivot, 6), (alpha, 3), (pivot, 7), (pivot, 8), (alpha, 4)):
-        forward(ring, k)
+    for k in range(4, H + 1):
+        forward(alpha, k // 2, (k % 2,))
+        forward(pivot, k)
+    forward(alpha, 4, (1,))
     arrive(pivot, H)
 
     for c in range(2):
@@ -241,9 +255,8 @@
         keep(block).start()
         return 0
 
-    def partial_beta(block, _):
-        bbuf[block] = combine(dot3((bth[...], btl[...]), rows_of(block), NT))
-        return 0
+    def partial_beta(block):
+        return combine(dot3((bth[...], btl[...]), rows_of(block), NT))
 
     def slot(q):
         return to_sibling(sbuf.at[q], re_out.at[q], uss.at[q], urs.at[q])
@@ -259,7 +272,6 @@
     forward(alpha, 6)
     ship(0)
     forward(alpha, 7)
-
     @pl.when(s == 0)
     def _():
         beta_over.wait_recv()
@@ -279,6 +291,12 @@
     panel_over.start()
     arrive(alpha, H)
     ship(3)
+
+    left = split(jnp.concatenate([al_all[mine, 0], al_all[mine, 1]], axis=0))
+    zr = dot3(left, (ph[0], plo[0]), NT)
+    zi = dot3(left, (ph[1], plo[1]), NT)
+    mult_ref[0] = zr[0:64] - zi[64:128]
+    mult_ref[1] = zi[0:64] + zr[64:128]
 
     panel_over.wait_recv()
     for b in range(4):
@@ -289,18 +307,13 @@
         bvh[:, b * 128 : (b + 1) * 128] = high
         bvl[:, b * 128 : (b + 1) * 128] = low
     lax.fori_loop(0, 4, form_beta, 0)
-    lax.fori_loop(0, BLOCKS, partial_beta, 0)
     for q in range(4):
-        sbeta[q] = bbuf[send[q]]
+        sbeta[q] = partial_beta(send[q])
     rest_over.start()
+    for p in range(4):
+        bbuf[p] = partial_beta(own[p])
     keep_beta = pltpu.make_async_copy(bbuf, ub_out, oss.at[BLOCKS])
     keep_beta.start()
-
-    left = split(jnp.concatenate([al_all[mine, 0], al_all[mine, 1]], axis=0))
-    zr = dot3(left, (ph[0], plo[0]), NT)
-    zi = dot3(left, (ph[1], plo[1]), NT)
-    mult_ref[0] = zr[0:64] - zi[64:128]
-    mult_ref[1] = zi[0:64] + zr[64:128]
 
     for ring in (pivot, alpha):
         for k in range(1, H + 1):
@@ -334,7 +347,7 @@
     reads, writes = [], []
     for p in range(4):
         own, slot = tab[p], tab[4 + p]
-        pairs = ((ue_ref.at[own], ue.at[p]), (re_ref.at[slot], re.at[p]), (ub_ref.at[own], ub.at[p]), (rb_ref.at[slot], rb.at[p]))
+        pairs = ((ue_ref.at[own], ue.at[p]), (re_ref.at[slot], re.at[p]), (ub_ref.at[p], ub.at[p]), (rb_ref.at[slot], rb.at[p]))
         reads.append([pltpu.make_async_copy(a, b, sems.at[p, i]) for i, (a, b) in enumerate(pairs)])
         for copy in reads[p]:
             copy.start()
@@ -372,13 +385,13 @@
         kernel,
         out_shape=(
             jax.ShapeDtypeStruct((BLOCKS, 2 * fx, 128), F32),
-            jax.ShapeDtypeStruct((BLOCKS, 2 * COLS, 128), F32),
+            jax.ShapeDtypeStruct((4, 2 * COLS, 128), F32),
             jax.ShapeDtypeStruct((4, 2 * fx, 128), F32),
             jax.ShapeDtypeStruct((4, 2 * COLS, 128), F32),
             jax.ShapeDtypeStruct((2, 64, width), F32),
             jax.ShapeDtypeStruct((8,), jnp.int32),
         ),
-        in_specs=[smem, vmem, hbm, vmem],
+        in_specs=[smem, hbm, hbm, hbm],
         out_specs=(hbm, hbm, hbm, hbm, vmem, smem),
         scratch_shapes=[
             pltpu.VMEM((N, 2, 32, width), F32),
@@ -386,6 +399,7 @@
             pltpu.VMEM((N, 32, 128), F32),
             pltpu.VMEM((N, 32, 128), F32),
             pltpu.VMEM((2, fx, width), F32),
+            pltpu.VMEM((2, 64, 2 * width), F32),
             pltpu.VMEM((N, 64, 128), F32),
             pltpu.VMEM((4, 2, 32, 128), F32),
             pltpu.VMEM((4, 2, 32, 128), F32),
@@ -401,11 +415,11 @@
             pltpu.VMEM((2 * COLS, width), BF16),
             pltpu.VMEM((2 * COLS, width), BF16),
             pltpu.VMEM((BLOCKS, 2 * fx, 128), F32),
-            pltpu.VMEM((BLOCKS, 2 * COLS, 128), F32),
+            pltpu.VMEM((4, 2 * COLS, 128), F32),
             pltpu.VMEM((4, 2 * fx, 128), F32),
             pltpu.VMEM((4, 2 * COLS, 128), F32),
             dma((2, 2, H)), dma((2, 2, H)), dma((2, 2, H)), dma((2, 2, H)),
-            dma((N,)), dma((N,)), dma((6,)), dma((6,)), dma((4,)), dma((4,)), dma((BLOCKS + 1,)), dma,
+            dma((N,)), dma((N,)), dma((6,)), dma((6,)), dma((4,)), dma((4,)), dma((BLOCKS + 1,)), dma((4,)),
         ],
         compiler_params=pltpu.CompilerParams(collective_id=0, has_side_effects=True, vmem_limit_bytes=56 * 2**20),
     )(face_blocks, pt, et, maps)

time: 114 us -> 112 us (0.982)
  no operation moved by 1% of the time
where the time goes in v4:
time: 112 us
  Pallas kernels  111 us (99%)
    pallas_call x1, Pallas kernels, per_device(): pl.pallas_call(kernel, out_shape=(jax.ShapeDtypeStruct((BLOCKS, 2 * fx, 1...  107 us
    pallas_call x1, Pallas kernels, per_device(): pl.pallas_call(place, in_specs=[smem] + [hbm] * 5, out_specs=(hbm,) * 3,...  3.73 us

profile of v4, /device:TPU:6, one launch (start us, length us, event | category | flops | bytes accessed | tf_op | source)
XLA Modules:
  0.0 111.8 jit_solution(9650249945435928703)
XLA Ops:
  0.6 107.4 %shard_map.67 = (f32[8,640,128]{2,1,0:T(8,128)}, f32[4,128,128]{2,1,0:T(8,128)}, f32[4,640,128]{2,1,0:T(8,128)}, f32[4,128,128]{2,1,0:T(8,128)}, f32[2,64,512]{2,1,0:T(8,128)}, /*index=5*/s32[8]{0:T(128)}) custom-call(s32[2,8]{1,0:T(2,128)} %faces_ref.1, f32[2,32,512]{2,1,0:T(8,128)} %bitcast.9, f32[2,320,512]{2,1,0:T(8,128)} %bitcast.7, f32[2,64,1024]{2,1,0:T(8,128)} %bitcast.8), custom_call_target="tpu_custom_call" | custom-call | tf_op jit(solution)/shard_map/pallas_call | solution.py:384
  108.1 3.7 %shard_map.68 = (f32[2,64,512]{2,1,0:T(8,128)}, f32[2,320,512]{2,1,0:T(8,128)}, f32[2,64,512]{2,1,0:T(8,128)}) custom-call(s32[8]{0:T(128)} %get-tuple-element.12.tab, f32[8,640,128]{2,1,0:T(8,128)} %get-tuple-element.13.ue_ref, f32[4,128,128]{2,1,0:T(8,128)} %get-tuple-element.14.ub_ref, f32[4,640,128]{2,1,0:T(8,128)} %get-tuple-element.15.re_ref, ...), custom_call_target="tpu_custom_call" | custom-call | tf_op jit(solution)/shard_map/pallas_call | solution.py:427

commit v5 on v4

--- a/solution.py
+++ b/solution.py
@@ -157,7 +157,7 @@
     alpha_over = [to_sibling(maps_in.at[c, :, width2], al_all.at[g, c], yss.at[4 + c], yrs.at[4 + c]) for c in range(2)]
     beta_over = to_sibling(pack, held, yss.at[1], yrs.at[1])
     panel_over = to_sibling(bsend, brecv, yss.at[2], yrs.at[2])
-    rest_over = to_sibling(sbeta, rb_out, yss.at[3], yrs.at[3])
+    rest_over = [to_sibling(sbeta.at[q], rb_out.at[q], yss.at[6 + q], yrs.at[6 + q]) for q in range(4)]
 
     @pl.when(s == 0)
     def _():
@@ -309,7 +309,7 @@
     lax.fori_loop(0, 4, form_beta, 0)
     for q in range(4):
         sbeta[q] = partial_beta(send[q])
-    rest_over.start()
+        rest_over[q].start()
     for p in range(4):
         bbuf[p] = partial_beta(own[p])
     keep_beta = pltpu.make_async_copy(bbuf, ub_out, oss.at[BLOCKS])
@@ -337,7 +337,7 @@
     panel_over.wait_send()
     for q in range(4):
         slot(q).wait()
-    rest_over.wait()
+        rest_over[q].wait()
 
 
 def place(tab, ue_ref, ub_ref, re_ref, rb_ref, mult_ref, schur_ref, ext_ref, out_ref, ue, ub, re, rb, mult, schur, ext, sems):
@@ -419,7 +419,7 @@
             pltpu.VMEM((4, 2 * fx, 128), F32),
             pltpu.VMEM((4, 2 * COLS, 128), F32),
             dma((2, 2, H)), dma((2, 2, H)), dma((2, 2, H)), dma((2, 2, H)),
-            dma((N,)), dma((N,)), dma((6,)), dma((6,)), dma((4,)), dma((4,)), dma((BLOCKS + 1,)), dma((4,)),
+            dma((N,)), dma((N,)), dma((10,)), dma((10,)), dma((4,)), dma((4,)), dma((BLOCKS + 1,)), dma((4,)),
         ],
         compiler_params=pltpu.CompilerParams(collective_id=0, has_side_effects=True, vmem_limit_bytes=56 * 2**20),
     )(face_blocks, pt, et, maps)

time: 112 us -> 112 us (level)
  no operation moved by 1% of the time
where the time goes in v5:
time: 112 us
  Pallas kernels  111 us (99%)
    pallas_call x1, Pallas kernels, per_device(): pl.pallas_call(kernel, out_shape=(jax.ShapeDtypeStruct((BLOCKS, 2 * fx, 1...  107 us
    pallas_call x1, Pallas kernels, per_device(): pl.pallas_call(place, in_specs=[smem] + [hbm] * 5, out_specs=(hbm,) * 3,...  3.73 us

profile of v5, /device:TPU:6, one launch (start us, length us, event | category | flops | bytes accessed | tf_op | source)
XLA Modules:
  0.0 111.9 jit_solution(8565204193403107378)
XLA Ops:
  0.6 107.5 %shard_map.67 = (f32[8,640,128]{2,1,0:T(8,128)}, f32[4,128,128]{2,1,0:T(8,128)}, f32[4,640,128]{2,1,0:T(8,128)}, f32[4,128,128]{2,1,0:T(8,128)}, f32[2,64,512]{2,1,0:T(8,128)}, /*index=5*/s32[8]{0:T(128)}) custom-call(s32[2,8]{1,0:T(2,128)} %faces_ref.1, f32[2,32,512]{2,1,0:T(8,128)} %bitcast.9, f32[2,320,512]{2,1,0:T(8,128)} %bitcast.7, f32[2,64,1024]{2,1,0:T(8,128)} %bitcast.8), custom_call_target="tpu_custom_call" | custom-call | tf_op jit(solution)/shard_map/pallas_call | solution.py:384
  108.1 3.7 %shard_map.68 = (f32[2,64,512]{2,1,0:T(8,128)}, f32[2,320,512]{2,1,0:T(8,128)}, f32[2,64,512]{2,1,0:T(8,128)}) custom-call(s32[8]{0:T(128)} %get-tuple-element.12.tab, f32[8,640,128]{2,1,0:T(8,128)} %get-tuple-element.13.ue_ref, f32[4,128,128]{2,1,0:T(8,128)} %get-tuple-element.14.ub_ref, f32[4,640,128]{2,1,0:T(8,128)} %get-tuple-element.15.re_ref, ...), custom_call_target="tpu_custom_call" | custom-call | tf_op jit(solution)/shard_map/pallas_call | solution.py:427
